TPU v7x, 768 devices: a whole 4x8x12 slice. The times are simulated.
768 devices in a mesh: lat: 48 (over z_lo, y, core), lon: 16 (over x, z_hi).
Axes of the slice: x: 4, y: 8, z: 12 (z_hi: 4, z_lo: 3; z = z_hi * 3 + z_lo), core: 2. Of those that a mesh axis runs over, the one named last changes fastest.
Arguments:
- fields: float32 [4, 6, 1536, 5120], P(None, None, 'lat', 'lon'), may hold values from -6 to 6
- dep_row: int32 [6, 1536, 5120], P(None, 'lat', 'lon'), may hold values from -4 to 1535, as said below
- dep_col: int32 [6, 1536, 5120], P(None, 'lat', 'lon'), may hold values from 0 to 5119, as said below
- weights: float32 [8, 6, 1536, 5120], P(None, None, 'lat', 'lon'), may hold values from -0.25 to 0.75
Outputs:
- departed: float32 [4, 6, 1536, 5120], P(None, None, 'lat', 'lon')
Inputs may be any that keep to these rules, and one draw needn't show every extreme that they name: dep_row[l, i, j] lies within i - 4 to i. dep_col[l, i, j] equals (j + k) modulo 5120 for some k from -4 to 0.
All inputs are finite; a program needn't handle non-finite values.
Results may differ from a plain program's by a relative error of at most 0.0003.
Values sent between devices are 32-bit elements; how exact they have to be, the bound alone decides.
A program may use at most 32 MiB of HBM per device.

v0:
```python
import jax
import jax.numpy as jnp
from jax import lax
from jax.sharding import PartitionSpec as P

HALO = 4


def padded_2(x, sides, width, wrap):
    for axis, dim in sides:
        devices, length = (lax.axis_size(axis), x.shape[dim])
        up = [(i, (i + 1) % devices) for i in range(devices if wrap else devices - 1)]
        down = [(j, i) for i, j in up]
        last = lax.slice_in_dim(x, length - width, length, axis=dim)
        leading = lax.slice_in_dim(x, 0, width, axis=dim)
        before = lax.ppermute(last, axis, up)
        after = lax.ppermute(leading, axis, down)
        x = jnp.concatenate([before, x, after], axis=dim)
    return x


def swapped(x, axis, stride):
    return lax.ppermute(x, axis, [(i, i ^ 1 << stride) for i in range(lax.axis_size(axis))])


def body(fields, dep_row, dep_col, weights):
    nfield, nlev, rows_here, cols_here = fields.shape
    lat_count = lax.axis_size("lat")
    lon_count = lax.axis_size("lon")
    band = lax.axis_index("lat")
    sector = lax.axis_index("lon")
    wide = padded_2(fields, (("lon", 3),), HALO, True)
    padded = padded_2(wide, (("lat", 2),), HALO, False)
    outgoing = jnp.where(band == 0, wide[:, :, :HALO], wide[:, :, rows_here - HALO :])
    partner = swapped(outgoing, "lon", lon_count.bit_length() - 2)
    flipped = partner[:, :, ::-1]
    north = jnp.where(band == 0, flipped, padded[:, :, :HALO])
    south = jnp.where(band == lat_count - 1, flipped, padded[:, :, rows_here + HALO :])
    padded = jnp.concatenate([north, padded[:, :, HALO : rows_here + HALO], south], axis=2)
    total_cols = cols_here * lon_count
    shape = (nlev, rows_here, cols_here)
    row_global = band * rows_here + lax.broadcasted_iota(jnp.int32, shape, 1)
    col_global = sector * cols_here + lax.broadcasted_iota(jnp.int32, shape, 2)
    offset_row = dep_row - row_global
    offset_col = jnp.mod(dep_col - col_global + HALO, total_cols) - HALO
    col_select = []
    row_select = []
    for shift in range(2 * HALO):
        col_term = jnp.zeros(shape, jnp.float32)
        row_term = jnp.zeros(shape, jnp.float32)
        for step in range(4):
            col_term = col_term + jnp.where(
                offset_col + step == shift - HALO, weights[4 + step], 0.0
            )
            row_term = row_term + jnp.where(offset_row + step == shift - HALO, weights[step], 0.0)
        col_select.append(col_term)
        row_select.append(row_term)
    total = jnp.zeros(fields.shape, jnp.float32)
    for row_shift in range(2 * HALO):
        band_rows = padded[:, :, row_shift : row_shift + rows_here]
        line = jnp.zeros(fields.shape, jnp.float32)
        for col_shift in range(2 * HALO):
            line = (
                line + col_select[col_shift] * band_rows[:, :, :, col_shift : col_shift + cols_here]
            )
        total = total + row_select[row_shift] * line
    return total


def solution(mesh):
    return jax.shard_map(
        body,
        mesh=mesh,
        in_specs=(
            P(None, None, "lat", "lon"),
            P(None, "lat", "lon"),
            P(None, "lat", "lon"),
            P(None, None, "lat", "lon"),
        ),
        out_specs=P(None, None, "lat", "lon"),
        check_vma=False,
    )
```

profile of v0, /device:TPU:25, one launch (start us, length us, event | category | flops | bytes accessed | tf_op | source)
XLA Modules:
  0.0 90.7 jit_solution(13914669216356076078)
XLA Ops:
  0.0 0.0 copy-start.4
  0.0 2.2 %fusion.131 = (f32[4,6,32,4]{3,2,1,0:T(8,128)}, f32[4,6,32,4]{3,2,1,0:T(8,128)}) fusion(f32[4,6,32,320]{3,2,1,0:T(8,128)} %param.4), kind=kLoop, calls=%fused_computation.271 | loop fusion | bytes 49152 | tf_op jit(solution)/shard_map/slice | solution.py:14
  2.2 7.6 %collective-permute-start = (f32[4,6,32,4]{3,2,1,0:T(8,128)}, f32[4,6,32,4]{3,2,1,0:T(8,128)}, u32[]{:S(2)}, u32[]{:S(2)}) collective-permute-start(f32[4,6,32,4]{3,2,1,0:T(8,128)} %get-tuple-element.26), channel_id=1, source_target_pairs={{0,1},{1,2},{2,3},{3,4},{4,5},{5,6},{6,7},{7,8},{8,9},{9,10},{10,1... | collective-permute-start | bytes 36872 | tf_op jit(solution)/shard_map/ppermute | solution.py:16
  9.8 10.8 %collective-permute-start.1 = (f32[4,6,32,4]{3,2,1,0:T(8,128)}, f32[4,6,32,4]{3,2,1,0:T(8,128)}, u32[]{:S(2)}, u32[]{:S(2)}) collective-permute-start(f32[4,6,32,4]{3,2,1,0:T(8,128)} %get-tuple-element.27), channel_id=1, source_target_pairs={{1,0},{2,1},{3,2},{4,3},{5,4},{6,5},{7,6},{8,7},{9,8},{10,9},{11,1... | collective-permute-start | bytes 36872 | tf_op jit(solution)/shard_map/ppermute | solution.py:17
  20.6 0.0 copy-done.4
  20.6 0.0 copy-start.1
  20.6 3.1 %fusion.83 = (f32[6,32,320]{2,1,0:T(8,128)}, f32[6,32,320]{2,1,0:T(8,128)}, f32[6,32,320]{2,1,0:T(8,128)}, f32[6,32,320]{2,1,0:T(8,128)}) fusion(f32[8,6,32,320]{3,2,1,0:T(8,128)} %param.7, s32[6,32,320]{2,1,0:T(8,128)S(1)} %copy-done.4, s32[320]{0:T(512)S(1)} %iota_add_fusion), kind=kLoop, calls=%fused_computation.158 | loop fusion | flops 3440640 | bytes 2213120 | tf_op jit(solution)/shard_map/add | solution.py:52
  23.7 0.0 copy-done.1
  23.7 1.7 %fusion.84 = (f32[6,32,320]{2,1,0:T(8,128)}, f32[6,32,320]{2,1,0:T(8,128)}, f32[6,32,320]{2,1,0:T(8,128)}, f32[6,32,320]{2,1,0:T(8,128)}) fusion(f32[8,6,32,320]{3,2,1,0:T(8,128)S(1)} %copy-done.1, s32[6,32,320]{2,1,0:T(8,128)S(1)} %copy-done.4, s32[320]{0:T(512)S(1)} %iota_add_fusion), kind=kLoop, calls=%fused_computation.159 | loop fusion | flops 3440640 | bytes 2213120 | tf_op jit(solution)/shard_map/add | solution.py:52
  25.3 0.0 copy-start
  25.3 2.6 %fusion.108 = (f32[6,32,320]{2,1,0:T(8,128)}, f32[6,32,320]{2,1,0:T(8,128)}, f32[6,32,320]{2,1,0:T(8,128)}, f32[6,32,320]{2,1,0:T(8,128)}) fusion(f32[8,6,32,320]{3,2,1,0:T(8,128)S(1)} %copy-done.1, s32[6,32,320]{2,1,0:T(8,128)} %param.5, s32[32]{0:T(128)S(1)} %iota_add_fusion.1), kind=kLoop, calls=%fused_computation.215 | loop fusion | flops 2949120 | bytes 2211968 | tf_op jit(solution)/shard_map/add | solution.py:55
  28.0 0.0 copy-start.5
  28.0 1.8 %collective-permute-done = f32[4,6,32,4]{3,2,1,0:T(8,128)} collective-permute-done((f32[4,6,32,4]{3,2,1,0:T(8,128)}, f32[4,6,32,4]{3,2,1,0:T(8,128)}, u32[]{:S(2)}, u32[]{:S(2)}) %collective-permute-start) | collective-permute-done | bytes 12320 | tf_op jit(solution)/shard_map/ppermute | solution.py:16
  29.7 14.6 %collective-permute-done.1 = f32[4,6,32,4]{3,2,1,0:T(8,128)} collective-permute-done((f32[4,6,32,4]{3,2,1,0:T(8,128)}, f32[4,6,32,4]{3,2,1,0:T(8,128)}, u32[]{:S(2)}, u32[]{:S(2)}) %collective-permute-start.1) | collective-permute-done | bytes 12320 | tf_op jit(solution)/shard_map/ppermute | solution.py:17
  44.4 0.0 copy-done
  44.4 2.1 %broadcast_select_fusion.2 = (f32[4,6,4,328]{3,2,1,0:T(4,128)}, f32[4,6,4,328]{3,2,1,0:T(4,128)}, f32[4,6,4,328]{3,2,1,0:T(4,128)}) fusion(pred[]{:T(512)S(6)} %eq.209, f32[4,6,32,4]{3,2,1,0:T(8,128)} %collective-permute-done.1, f32[4,6,32,320]{3,2,1,0:T(8,128)S(1)} %copy-done, f32[4,6,32,4]{3,2,1,0:T(8,128)} %collective-permute-done), kind=kLoop, calls=%fused_computation.268 | loop fusion | flops 157440 | bytes 1385473 | tf_op jit(solution)/shard_map/jit(_where)/select_n | solution.py:34
  46.4 4.7 %collective-permute-start.2 = (f32[4,6,4,328]{3,2,1,0:T(4,128)}, f32[4,6,4,328]{3,2,1,0:T(4,128)S(1)}, u32[]{:S(2)}, u32[]{:S(2)}) collective-permute-start(f32[4,6,4,328]{3,2,1,0:T(4,128)} %get-tuple-element.5), channel_id=1, source_target_pairs={{0,8},{1,9},{2,10},{3,11},{4,12},{5,13},{6,14},{7,15},{8,0},{9,1},... | collective-permute-start | bytes 377864 | tf_op jit(solution)/shard_map/ppermute | solution.py:23
  51.1 6.2 %collective-permute-start.3 = (f32[4,6,4,328]{3,2,1,0:T(4,128)}, f32[4,6,4,328]{3,2,1,0:T(4,128)S(1)}, u32[]{:S(2)}, u32[]{:S(2)}) collective-permute-start(f32[4,6,4,328]{3,2,1,0:T(4,128)} %get-tuple-element.6), channel_id=1, source_target_pairs={{0,16},{16,32},{32,48},{48,64},{64,80},{80,96},{96,112},{112,128},... | collective-permute-start | bytes 377864 | tf_op jit(solution)/shard_map/ppermute | solution.py:16
  57.3 1.9 %collective-permute-start.4 = (f32[4,6,4,328]{3,2,1,0:T(4,128)}, f32[4,6,4,328]{3,2,1,0:T(4,128)S(1)}, u32[]{:S(2)}, u32[]{:S(2)}) collective-permute-start(f32[4,6,4,328]{3,2,1,0:T(4,128)} %get-tuple-element.7), channel_id=1, source_target_pairs={{16,0},{32,16},{48,32},{64,48},{80,64},{96,80},{112,96},{128,112},... | collective-permute-start | bytes 377864 | tf_op jit(solution)/shard_map/ppermute | solution.py:17
  59.3 0.0 copy-done.5
  59.3 1.6 %fusion.107 = (f32[6,32,320]{2,1,0:T(8,128)}, f32[6,32,320]{2,1,0:T(8,128)}, f32[6,32,320]{2,1,0:T(8,128)}, f32[6,32,320]{2,1,0:T(8,128)}) fusion(f32[8,6,32,320]{3,2,1,0:T(8,128)S(1)} %copy-done.1, s32[6,32,320]{2,1,0:T(8,128)S(1)} %copy-done.5, s32[32]{0:T(128)S(1)} %iota_add_fusion.1), kind=kLoop, calls=%fused_computation.214 | loop fusion | flops 2949120 | bytes 2211968 | tf_op jit(solution)/shard_map/add | solution.py:55
  60.8 0.0 collective-permute-done.2
  60.8 0.3 rev.3
  61.1 0.0 collective-permute-done.3
  61.1 4.1 %collective-permute-done.4 = f32[4,6,4,328]{3,2,1,0:T(4,128)S(1)} collective-permute-done((f32[4,6,4,328]{3,2,1,0:T(4,128)}, f32[4,6,4,328]{3,2,1,0:T(4,128)S(1)}, u32[]{:S(2)}, u32[]{:S(2)}) %collective-permute-start.4) | collective-permute-done | bytes 125984 | tf_op jit(solution)/shard_map/ppermute | solution.py:17
  65.2 0.0 copy-start.2
  65.2 0.0 copy-start.3
  65.3 3.1 %maximum_maximum_fusion = (f32[4,6,36,328]{3,2,1,0:T(8,128)S(1)}, f32[4,6,36,328]{3,2,1,0:T(8,128)S(1)}) fusion(f32[4,6,32,4]{3,2,1,0:T(8,128)} %collective-permute-done.1, f32[4,6,32,320]{3,2,1,0:T(8,128)} %param.4, f32[4,6,32,4]{3,2,1,0:T(8,128)} %collective-permute-done, f32[4,6,4,328]{3,2,1,0:T(4,128)S(1)} %bitcast.269, f32[4,6,4,328]{3,2,1,0:T(4,128)S(1)} %bitcast.270), kind=kLoop, calls=%fused_computation.5 | loop fusion | flops 1700352 | bytes 3526656 | tf_op jit(solution)/shard_map/concatenate | solution.py:39
  68.4 0.0 copy-done.2
  68.4 0.0 copy-done.3
  68.4 22.3 %fusion.8 = f32[4,6,32,320]{3,2,1,0:T(8,128)} fusion(f32[4,6,32,4]{3,2,1,0:T(8,128)} %collective-permute-done.1, f32[4,6,32,4]{3,2,1,0:T(8,128)} %collective-permute-done, f32[4,6,36,328]{3,2,1,0:T(8,128)S(1)} %get-tuple-element.25, f32[4,6,32,320]{3,2,1,0:T(8,128)} %param.4, f32[4,6,36,328]{3,2,1,0:T(8,128)S(1)} %get-tuple-element.24, ...), kind=kLoop, calls=%fused_computation.15 | loop fusion | flops 34897920 | bytes 60973056 | tf_op jit(solution)/shard_map/add | solution.py:66
  (3 shorter events, 0.0 us)
Async XLA Ops:
  0.0 20.6 %copy-start.4 = (s32[6,32,320]{2,1,0:T(8,128)S(1)}, s32[6,32,320]{2,1,0:T(8,128)}, u32[]{:S(2)}) copy-start(s32[6,32,320]{2,1,0:T(8,128)} %param.6) | copy-start | bytes 737284
  2.2 27.6 %collective-permute-start = (f32[4,6,32,4]{3,2,1,0:T(8,128)}, f32[4,6,32,4]{3,2,1,0:T(8,128)}, u32[]{:S(2)}, u32[]{:S(2)}) collective-permute-start(f32[4,6,32,4]{3,2,1,0:T(8,128)} %get-tuple-element.26), channel_id=1, source_target_pairs={{0,1},{1,2},{2,3},{3,4},{4,5},{5,6},{6,7},{7,8},{8,9},{9,10},{10,1... | collective-permute-start | bytes 36872 | tf_op jit(solution)/shard_map/ppermute | solution.py:16
  9.8 34.6 %collective-permute-start.1 = (f32[4,6,32,4]{3,2,1,0:T(8,128)}, f32[4,6,32,4]{3,2,1,0:T(8,128)}, u32[]{:S(2)}, u32[]{:S(2)}) collective-permute-start(f32[4,6,32,4]{3,2,1,0:T(8,128)} %get-tuple-element.27), channel_id=1, source_target_pairs={{1,0},{2,1},{3,2},{4,3},{5,4},{6,5},{7,6},{8,7},{9,8},{10,9},{11,1... | collective-permute-start | bytes 36872 | tf_op jit(solution)/shard_map/ppermute | solution.py:17
  20.6 3.1 %copy-start.1 = (f32[8,6,32,320]{3,2,1,0:T(8,128)S(1)}, f32[8,6,32,320]{3,2,1,0:T(8,128)}, u32[]{:S(2)}) copy-start(f32[8,6,32,320]{3,2,1,0:T(8,128)} %param.7) | copy-start | bytes 5898244
  25.3 19.0 %copy-start = (f32[4,6,32,320]{3,2,1,0:T(8,128)S(1)}, f32[4,6,32,320]{3,2,1,0:T(8,128)}, u32[]{:S(2)}) copy-start(f32[4,6,32,320]{3,2,1,0:T(8,128)} %param.4) | copy-start | bytes 2949124
  28.0 31.3 %copy-start.5 = (s32[6,32,320]{2,1,0:T(8,128)S(1)}, s32[6,32,320]{2,1,0:T(8,128)}, u32[]{:S(2)}) copy-start(s32[6,32,320]{2,1,0:T(8,128)} %param.5) | copy-start | bytes 737284
  46.4 14.4 %collective-permute-start.2 = (f32[4,6,4,328]{3,2,1,0:T(4,128)}, f32[4,6,4,328]{3,2,1,0:T(4,128)S(1)}, u32[]{:S(2)}, u32[]{:S(2)}) collective-permute-start(f32[4,6,4,328]{3,2,1,0:T(4,128)} %get-tuple-element.5), channel_id=1, source_target_pairs={{0,8},{1,9},{2,10},{3,11},{4,12},{5,13},{6,14},{7,15},{8,0},{9,1},... | collective-permute-start | bytes 377864 | tf_op jit(solution)/shard_map/ppermute | solution.py:23
  51.1 10.0 %collective-permute-start.3 = (f32[4,6,4,328]{3,2,1,0:T(4,128)}, f32[4,6,4,328]{3,2,1,0:T(4,128)S(1)}, u32[]{:S(2)}, u32[]{:S(2)}) collective-permute-start(f32[4,6,4,328]{3,2,1,0:T(4,128)} %get-tuple-element.6), channel_id=1, source_target_pairs={{0,16},{16,32},{32,48},{48,64},{64,80},{80,96},{96,112},{112,128},... | collective-permute-start | bytes 377864 | tf_op jit(solution)/shard_map/ppermute | solution.py:16
  57.3 7.9 %collective-permute-start.4 = (f32[4,6,4,328]{3,2,1,0:T(4,128)}, f32[4,6,4,328]{3,2,1,0:T(4,128)S(1)}, u32[]{:S(2)}, u32[]{:S(2)}) collective-permute-start(f32[4,6,4,328]{3,2,1,0:T(4,128)} %get-tuple-element.7), channel_id=1, source_target_pairs={{16,0},{32,16},{48,32},{64,48},{80,64},{96,80},{112,96},{128,112},... | collective-permute-start | bytes 377864 | tf_op jit(solution)/shard_map/ppermute | solution.py:17
  65.2 3.1 %copy-start.2 = (f32[6,32,320]{2,1,0:T(8,128)S(1)}, f32[6,32,320]{2,1,0:T(8,128)}, u32[]{:S(2)}) copy-start(f32[6,32,320]{2,1,0:T(8,128)} %get-tuple-element.8) | copy-start | bytes 737284
  65.2 3.1 %copy-start.3 = (f32[6,32,320]{2,1,0:T(8,128)S(1)}, f32[6,32,320]{2,1,0:T(8,128)}, u32[]{:S(2)}) copy-start(f32[6,32,320]{2,1,0:T(8,128)} %get-tuple-element.9) | copy-start | bytes 737284
where the time goes:
time: 91 us; the launch traced here: 90.7 us
  other arithmetic  36.4 us (40%)
  starting transfers between devices  31.2 us (34%)
  waiting for transfers between devices  20.5 us (23%)
  local copies, waits for them, and re-layouts  2.45 us (3%)
    add x1, other arithmetic, body(): total = total + row_select[row_shift] * line  22.3 us
    ppermute x2, waiting for transfers between devices, padded_2(): after = lax.ppermute(leading, axis, down)  18.7 us
    ppermute x2, starting transfers between devices, padded_2(): before = lax.ppermute(last, axis, up)  13.8 us
    ppermute x2, starting transfers between devices, padded_2(): after = lax.ppermute(leading, axis, down)  12.7 us
    add x2, other arithmetic, body(): col_term + jnp.where(offset_col + step == shift - HALO, weights[4 + step]...  4.73 us
    ppermute x1, starting transfers between devices, swapped(): lax.ppermute(x, axis, [(i, i ^ 1 << stride) for i in range(lax.axis_size(...  4.71 us
    add x2, other arithmetic, body(): row_term + jnp.where(offset_row + step == shift - HALO, weights[step], 0.0)  4.18 us
    concatenate x1, other arithmetic, body(): jnp.concatenate([north, padded[:, :, HALO:rows_here + HALO], south], axis=2)  3.11 us
  transfers between devices with their start and end apart: 5, of which 3 were waited for; matrix products, arithmetic and copies ran while one was open for 10% of the time, Pallas kernels for 0%

commit v1 on v0

v1 whole, which is shorter than its diff:
```python
import functools

import jax
import jax.numpy as jnp
from jax import lax
from jax.experimental import pallas as pl
from jax.experimental.pallas import tpu as pltpu
from jax.sharding import PartitionSpec as P

MESH = pl.DeviceIdType.MESH
F32 = jnp.float32
LANES = 128
SUB = 8
HALO = 4
SPAN = 2 * HALO
EARLY_EVERY = 4


def lane_iota(shape):
    return lax.broadcasted_iota(jnp.int32, shape, len(shape) - 1)


def sub_iota(shape):
    return lax.broadcasted_iota(jnp.int32, shape, len(shape) - 2)


def roll(x, shift, axis):
    size = x.shape[axis]
    return pltpu.roll(x, shift % size, axis) if shift % size else x


def widen(x):
    width = x.shape[-1]
    if width == LANES:
        return x
    return jnp.concatenate([x, jnp.zeros(x.shape[:-1] + (LANES - width,), x.dtype)], axis=-1)


def neighbours(band, sector, nband, nsector):
    east = lax.rem(sector + 1, nsector)
    west = lax.rem(sector + nsector - 1, nsector)
    top, bottom = band == 0, band == nband - 1
    north, south = jnp.where(top, band, band - 1), jnp.where(bottom, band, band + 1)
    half = nsector // 2
    turn_n, turn_s = jnp.where(top, half, 0), jnp.where(bottom, half, 0)

    def at(row, col, turn):
        return (row, lax.rem(col + turn, nsector))

    return {
        "E": (band, east), "W": (band, west),
        "N": at(north, sector, turn_n), "S": at(south, sector, turn_s),
        "NE": at(north, east, turn_n), "NW": at(north, west, turn_n),
        "SE": at(south, east, turn_s), "SW": at(south, west, turn_s),
    }


def select_weights(offset, taps):
    masks = [offset == o for o in range(HALO + 1)]
    out = []
    for s in range(SPAN):
        term = jnp.zeros(offset.shape, F32)
        for a in range(4):
            if 0 <= s - a <= HALO:
                term = jnp.where(masks[s - a], taps[a], term)
        out.append(term)
    return out


def flip4(x):
    i = sub_iota(x.shape)
    x = jnp.where((i & 1) == 1, roll(x, 1, 0), roll(x, -1, 0))
    return jnp.where((i & 2) == 2, roll(x, 2, 0), roll(x, -2, 0))


def kernel(dims, fields, dep_row, dep_col, weights, out,
           fv, drv, dcv, wv, ov, rc, sh, slab, slab_in, strip, strip_in, corner, corner_in,
           tn, xx, pw, pd, in_sem, out_sem, send_sem, recv_sem):
    nf, nl, rows, cols, nband, nsector, total_cols = dims
    band, sector = lax.axis_index("lat"), lax.axis_index("lon")
    there = neighbours(band, sector, nband, nsector)
    top, bottom = band == 0, band == nband - 1
    tiles = pl.cdiv(cols, LANES)
    tail = cols - (tiles - 1) * LANES
    widths = [LANES] * (tiles - 1) + [tail]
    blocks = rows // SUB
    last = rows - SUB
    lane = lane_iota((SUB, LANES))
    sub = sub_iota((SUB, LANES))

    loads = [pltpu.make_async_copy(fields, fv, in_sem.at[0]),
             pltpu.make_async_copy(dep_row, drv, in_sem.at[1]),
             pltpu.make_async_copy(dep_col, dcv, in_sem.at[2]),
             pltpu.make_async_copy(weights, wv, in_sem.at[3])]
    for copy in loads:
        copy.start()
    barrier = pltpu.get_barrier_semaphore()
    for name in there:
        pl.semaphore_signal(barrier, inc=1, device_id=there[name], device_id_type=MESH)

    def tile(ref, lead, start, c):
        return ref[lead + (slice(start, start + SUB), slice(c * LANES, c * LANES + widths[c]))]

    loads[0].wait()
    for k in range(blocks):
        east = jnp.zeros((SUB, LANES), F32)
        west = jnp.zeros((SUB, LANES), F32)
        for f in range(nf):
            for l in range(nl):
                p = HALO * (f * nl + l)
                own = (lane >= p) & (lane < p + HALO)
                e = widen(tile(fv, (f, l), SUB * k, tiles - 1))
                east = jnp.where(own, roll(e, p - (tail - HALO), 1), east)
                west = jnp.where(own, roll(tile(fv, (f, l), SUB * k, 0), p, 1), west)
        strip[0, pl.ds(SUB * k, SUB), :] = east
        strip[1, pl.ds(SUB * k, SUB), :] = west

    def slab_of(side, g, l, c):
        a = tile(fv, (2 * g, l), 0 if side == 0 else last, c)
        b = tile(fv, (2 * g + 1, l), 0 if side == 0 else last, c)
        mask = sub_iota(a.shape) < HALO
        return jnp.where(mask, a, roll(b, HALO, 0)) if side == 0 else jnp.where(mask, roll(a, HALO, 0), b)

    for side in range(2):
        for l in range(nl):
            for c in range(tiles - 1):
                for g in range(2):
                    slab[side, l, 2 * c + g] = slab_of(side, g, l, c)
            pair = [slab_of(side, g, l, tiles - 1) for g in range(2)]
            slab[side, l, 2 * tiles - 2] = jnp.concatenate(pair, axis=-1)
    for edge in range(2):
        corner[0, edge] = strip[edge, 0:SUB, :]
        corner[1, edge] = roll(strip[edge, pl.ds(last, SUB), :], HALO, 0)

    for side, here in ((0, top), (1, bottom)):
        @pl.when(here)
        def _():
            for l in range(nl):
                for m in range(2 * tiles - 1):
                    slab[side, l, m] = flip4(slab[side, l, m])
            for edge in range(2):
                corner[side, edge] = flip4(corner[side, edge])

    for copy in loads[1:]:
        copy.wait()

    def zero_pads():
        for c in range(tiles):
            for f in range(nf):
                for t in range(SPAN):
                    sh[c, f, t, 0:SUB, :] = jnp.zeros((SUB, LANES), F32)
                    sh[c, f, t, pl.ds(SUB + rows, SUB), :] = jnp.zeros((SUB, LANES), F32)
        for m in range(2 * tiles - 1):
            for side in range(2):
                for t in range(SPAN):
                    tn[side, m, t, 0:SUB, :] = jnp.zeros((SUB, LANES), F32)
                    tn[side, m, t, 2 * SUB:3 * SUB, :] = jnp.zeros((SUB, LANES), F32)
        pw[...] = jnp.zeros(pw.shape, F32)

    def shifted(mid, left, right, t):
        d = t - HALO
        if d == 0:
            return mid
        if d < 0:
            return roll(mid if left is None else jnp.where(lane >= LANES + d, left, mid), -d, 1) if left is not None else jnp.where(
                lane < -d, 0.0, roll(mid, -d, 1))
        if right is None:
            return jnp.where(lane >= LANES - d, 0.0, roll(mid, -d, 1))
        return roll(jnp.where(lane < d, right, mid), -d, 1)

    def main():
        zero_pads()

        @pl.loop(0, nl)
        def _(l):
            for c in range(tiles):
                shape = (SUB, widths[c])
                ones = slice(0, widths[c])
                for k in range(blocks):
                    at = (l, slice(SUB * k, SUB * k + SUB), slice(c * LANES, c * LANES + widths[c]))
                    o_row = drv[at] - (band * rows + SUB * k - HALO + sub_iota(shape))
                    o_col = dcv[at] - (sector * cols + c * LANES - HALO + lane_iota(shape))
                    o_col = jnp.where(o_col > HALO, o_col - total_cols, o_col)
                    row_w = select_weights(o_row, [wv[(a,) + at] for a in range(4)])
                    col_w = select_weights(o_col, [wv[(4 + a,) + at] for a in range(4)])
                    for s in range(SPAN):
                        rc[l, c, s, pl.ds(SUB * k, SUB), ones] = row_w[s]
                        rc[l, c, SPAN + s, pl.ds(SUB * k, SUB), ones] = col_w[s]
                    if c == 0 or c == tiles - 1:
                        side = 0 if c == 0 else 1
                        own = (lane >= HALO * l) & (lane < HALO * l + HALO)
                        for i, x in enumerate(row_w + col_w):
                            x = widen(x)
                            if side:
                                x = roll(x, -(tail - HALO), 1)
                            x = pltpu.roll(x, HALO * l, 1)
                            spot = (side, i, pl.ds(SUB * k, SUB), slice(None))
                            pw[spot] = jnp.where(own, x, pw[spot])
                for f in range(nf):
                    for k in range(blocks):
                        mid = widen(tile(fv, (f, l), SUB * k, c))
                        left = tile(fv, (f, l), SUB * k, c - 1) if c else None
                        right = widen(tile(fv, (f, l), SUB * k, c + 1)) if c + 1 < tiles else None
                        for t in range(SPAN):
                            sh[c, f, t, pl.ds(SUB + SUB * k, SUB), :] = shifted(mid, left, right, t)
                col_t = [[rc[l, c, SPAN + t, pl.ds(k, SUB, stride=blocks), :] for t in range(SPAN)] for k in range(blocks)]
                for f in range(nf):
                    acc = [None] * blocks
                    for u in range(SPAN + blocks - 1):
                        x = [sh[c, f, t, pl.ds(HALO + u, SUB, stride=blocks), :] for t in range(SPAN)]
                        for k in range(blocks):
                            s = u - k
                            if 0 <= s < SPAN:
                                line = col_t[k][0] * x[0]
                                for t in range(1, SPAN):
                                    line = line + col_t[k][t] * x[t]
                                line = line * rc[l, c, s, pl.ds(k, SUB, stride=blocks), :]
                                acc[k] = line if acc[k] is None else acc[k] + line
                    for k in range(blocks):
                        ov[f, l, c, pl.ds(k, SUB, stride=blocks), :] = acc[k]

        for side in range(2):
            for i in range(2 * SPAN):
                for k in range(blocks):
                    spot = (side, i, pl.ds(SUB * k, SUB), slice(None))
                    x = pw[spot]
                    x = x + roll(x, HALO * nl, 1)
                    pw[spot] = x + roll(x, 2 * HALO * nl, 1)

    early = lax.rem(sector, EARLY_EVERY) == 0

    @pl.when(early)
    def _():
        main()

    pl.semaphore_wait(barrier, len(there))
    slot_n, slot_s = jnp.where(top, 0, 1), jnp.where(bottom, 1, 0)
    sends = []

    def send(src, dst, i, j, to):
        copy = pltpu.make_async_remote_copy(
            src_ref=src, dst_ref=dst, send_sem=send_sem.at[i], recv_sem=recv_sem.at[j],
            device_id=there[to], device_id_type=MESH)
        copy.start()
        sends.append(copy)

    send(strip.at[0], strip_in.at[0], 0, 0, "E")
    send(strip.at[1], strip_in.at[1], 1, 1, "W")
    for side, slot, names in ((0, slot_n, ("NE", "NW")), (1, slot_s, ("SE", "SW"))):
        for edge in range(2):
            n = 2 * side + edge
            send(corner.at[side, edge, pl.ds(0, HALO)], corner_in.at[slot, edge, pl.ds(0, HALO)], 2 + n, 2 + 2 * slot + edge, names[edge])
    send(slab.at[0], slab_in.at[slot_n], 6, 6 + slot_n, "N")
    send(slab.at[1], slab_in.at[slot_s], 7, 6 + slot_s, "S")

    @pl.when(jnp.logical_not(early))
    def _():
        main()

    def landed(ref, j):
        pltpu.make_async_copy(ref, ref, recv_sem.at[j]).wait()

    landed(slab_in.at[0], 6)
    landed(slab_in.at[1], 7)
    group = sub & (HALO - 1)

    def both(x, side):
        return jnp.where(sub < HALO, x, roll(x, HALO, 0)) if side == 0 else jnp.where(sub < HALO, roll(x, HALO, 0), x)

    @pl.loop(0, nl)
    def _(l):
        for side in range(2):
            base = 0 if side == 0 else last
            shifts = range(HALO) if side == 0 else range(HALO + 1, SPAN)
            ends = [slab_in[side, l, 2 * tiles - 2]] * 2
            ends[1] = roll(ends[1], -(LANES - tail), 1)
            for m in range(2 * tiles - 1):
                c, g = m // 2, m % 2
                mid = slab_in[side, l, m]
                for t in range(SPAN):
                    d = t - HALO
                    if c < tiles - 1:
                        left = slab_in[side, l, m - 2] if c else None
                        right = (slab_in[side, l, m + 2] if c + 2 < tiles else ends[g])
                        x = shifted(mid, left, right, t)
                    elif d <= 0:
                        x = roll(mid, -d, 1)
                        for h in range(2):
                            lo = h * (LANES - tail)
                            x = jnp.where((lane >= lo) & (lane < lo - d), roll(slab_in[side, l, m - 2 + h], lo - d, 1), x) if d else x
                    else:
                        inner = lane & (LANES // 2 - 1)
                        x = jnp.where(inner >= LANES // 2 - d, 0.0, roll(mid, -d, 1))
                    tn[side, m, t, SUB:2 * SUB, :] = x
            for c in range(tiles):
                def weight(i):
                    x = rc[l, c, i, pl.ds(base, SUB), 0:widths[c]]
                    if c == tiles - 1:
                        x = jnp.concatenate([x, x], axis=-1)
                    return both(x, side)

                col_w = [weight(SPAN + t) for t in range(SPAN)]
                row_w = {}
                for s in shifts:
                    valid = group + s < HALO if side == 0 else group + s >= SPAN
                    row_w[s] = jnp.where(valid, weight(s), 0.0)
                for g in range(2 if c < tiles - 1 else 1):
                    m = 2 * c + g
                    acc = None
                    for s in shifts:
                        first = SUB + s if side == 0 else s
                        line = None
                        for t in range(SPAN):
                            term = col_w[t] * tn[side, m, t, pl.ds(first, SUB), :]
                            line = term if line is None else line + term
                        line = line * row_w[s]
                        acc = line if acc is None else acc + line
                    keep = sub < HALO if side == 0 else sub >= HALO
                    for h in range(2 if c < tiles - 1 else 4):
                        part = acc
                        f = 2 * g + h if c < tiles - 1 else h
                        if c == tiles - 1 and h >= 2:
                            part = roll(part, -(LANES - tail), 1)
                        if side == 0:
                            part = part if f % 2 == 0 else roll(part, HALO, 0)
                        else:
                            part = part if f % 2 == 1 else roll(part, HALO, 0)
                        spot = (f, l, c, pl.ds(base, SUB), slice(None))
                        ov[spot] = ov[spot] + jnp.where(keep, part, 0.0)

    landed(strip_in.at[0], 0)
    landed(strip_in.at[1], 1)
    for side in range(2):
        for edge in range(2):
            landed(corner_in.at[side, edge, pl.ds(0, HALO)], 2 + 2 * side + edge)
    for edge in range(2):
        taps = range(HALO) if edge == 0 else range(HALO + 1, SPAN)
        for t in taps:
            d = t if edge == 0 else t - SPAN
            for k in range(blocks):
                xx[edge, t, pl.ds(SUB + SUB * k, SUB), :] = roll(strip_in[edge, pl.ds(SUB * k, SUB), :], -d, 1)
            xx[edge, t, HALO:SUB, :] = roll(corner_in[0, edge, 0:HALO, :], -d, 1)
            xx[edge, t, SUB + rows:SUB + rows + HALO, :] = roll(corner_in[1, edge, 0:HALO, :], -d, 1)
        col = lane & (HALO - 1)
        for k in range(blocks):
            col_w = {}
            for t in taps:
                valid = col + t < HALO if edge == 0 else col + t >= SPAN
                col_w[t] = jnp.where(valid, pw[edge, SPAN + t, pl.ds(k, SUB, stride=blocks), :], 0.0)
            acc = None
            for s in range(SPAN):
                line = None
                for t in taps:
                    term = col_w[t] * xx[edge, t, pl.ds(HALO + k + s, SUB, stride=blocks), :]
                    line = term if line is None else line + term
                line = line * pw[edge, s, pl.ds(k, SUB, stride=blocks), :]
                acc = line if acc is None else acc + line
            pd[edge, pl.ds(k, SUB, stride=blocks), :] = acc
    copies = []
    for f in range(nf):
        for l in range(nl):
            p = HALO * (f * nl + l)
            for k in range(blocks):
                at = pl.ds(SUB * k, SUB)
                for c in range(tiles):
                    x = ov[f, l, c, at, :]
                    if c == 0:
                        x = x + jnp.where(lane < HALO, roll(pd[0, at, :], -p, 1), 0.0)
                    if c == tiles - 1:
                        keep = (lane >= tail - HALO) & (lane < tail)
                        x = x + jnp.where(keep, roll(pd[1, at, :], tail - HALO - p, 1), 0.0)
                    fv[f, l, at, c * LANES:c * LANES + widths[c]] = x[:, :widths[c]]
        copy = pltpu.make_async_copy(fv.at[f], out.at[f], out_sem.at[f])
        copy.start()
        copies.append(copy)
    for copy in copies:
        copy.wait()
    for copy in sends:
        copy.wait_send()


def solution(mesh):
    nband, nsector = mesh.shape["lat"], mesh.shape["lon"]

    def body(fields, dep_row, dep_col, weights):
        nf, nl, rows, cols = fields.shape
        tiles = pl.cdiv(cols, LANES)
        dims = (nf, nl, rows, cols, nband, nsector, cols * nsector)
        vmem = lambda *shape: pltpu.VMEM(shape, F32)
        groups = 2 * tiles - 1
        return pl.pallas_call(
            functools.partial(kernel, dims),
            out_shape=jax.ShapeDtypeStruct(fields.shape, F32),
            in_specs=[pl.BlockSpec(memory_space=pltpu.HBM)] * 4,
            out_specs=pl.BlockSpec(memory_space=pltpu.HBM),
            scratch_shapes=[
                vmem(nf, nl, rows, cols),
                pltpu.VMEM((nl, rows, cols), jnp.int32),
                pltpu.VMEM((nl, rows, cols), jnp.int32),
                vmem(8, nl, rows, cols),
                vmem(nf, nl, tiles, rows, LANES),
                vmem(nl, tiles, 2 * SPAN, rows, LANES),
                vmem(tiles, nf, SPAN, rows + 2 * SUB, LANES),
                vmem(2, nl, groups, SUB, LANES), vmem(2, nl, groups, SUB, LANES),
                vmem(2, rows, LANES), vmem(2, rows, LANES),
                vmem(2, 2, SUB, LANES), vmem(2, 2, SUB, LANES),
                vmem(2, groups, SPAN, 3 * SUB, LANES),
                vmem(2, SPAN, rows + 2 * SUB, LANES),
                vmem(2, 2 * SPAN, rows, LANES),
                vmem(2, rows, LANES),
                pltpu.SemaphoreType.DMA((4,)), pltpu.SemaphoreType.DMA((nf,)),
                pltpu.SemaphoreType.DMA((8,)), pltpu.SemaphoreType.DMA((8,)),
            ],
            compiler_params=pltpu.CompilerParams(
                collective_id=0, has_side_effects=True, vmem_limit_bytes=67043328),
            name="advect",
        )(fields, dep_row, dep_col, weights)

    return jax.shard_map(
        body,
        mesh=mesh,
        in_specs=(
            P(None, None, "lat", "lon"),
            P(None, "lat", "lon"),
            P(None, "lat", "lon"),
            P(None, None, "lat", "lon"),
        ),
        out_specs=P(None, None, "lat", "lon"),
        check_vma=False,
    )
```

time: 91 us -> 30.4 us (0.33)
  the two profiles are of different devices: /device:TPU:25 before, /device:TPU:4 now
where the time goes in v1:
time: 30.4 us; the launch traced here: 30.2 us
  Pallas kernels  27.9 us (92%)
  local copies, waits for them, and re-layouts  2.36 us (8%)
    pallas_call x1, Pallas kernels, body(): pl.pallas_call(functools.partial(kernel, dims), out_shape=jax.ShapeDtypeS...  27.9 us
    unnamed x1, local copies, waits for them, and re-layouts  2.36 us

profile of v1, /device:TPU:4, one launch (start us, length us, event | category | flops | bytes accessed | tf_op | source)
XLA Modules:
  0.0 30.2 jit_solution(13463150384601795580)
XLA Ops:
  0.0 27.9 %advect.1 = f32[4,6,32,320]{3,2,1,0:T(8,128)} custom-call(f32[4,6,32,320]{3,2,1,0:T(8,128)} %fields.1, s32[6,32,320]{2,1,0:T(8,128)} %dep_row.1, s32[6,32,320]{2,1,0:T(8,128)} %dep_col.1, f32[8,6,32,320]{3,2,1,0:T(8,128)} %weights.1), custom_call_target="tpu_custom_call" | custom-call | tf_op jit(solution)/shard_map/advect/pallas_call | solution.py:391
  27.9 2.4 %copy.6 = f32[4,6,32,320]{3,2,1,0:T(8,128)} copy(f32[4,6,32,320]{3,2,1,0:T(8,128)} %advect.1) | data formatting | bytes 1966080

commit v2 on v1

--- a/solution.py
+++ b/solution.py
@@ -13,7 +13,8 @@
 SUB = 8
 HALO = 4
 SPAN = 2 * HALO
-EARLY_EVERY = 4
+RUN = 4
+PIECES = 3
 
 
 def lane_iota(shape):
@@ -75,7 +76,7 @@
 
 def kernel(dims, fields, dep_row, dep_col, weights, out,
            fv, drv, dcv, wv, ov, rc, sh, slab, slab_in, strip, strip_in, corner, corner_in,
-           tn, xx, pw, pd, in_sem, out_sem, send_sem, recv_sem):
+           tn, nw, xx, pw, pd, in_sem, send_sem, recv_sem):
     nf, nl, rows, cols, nband, nsector, total_cols = dims
     band, sector = lax.axis_index("lat"), lax.axis_index("lon")
     there = neighbours(band, sector, nband, nsector)
@@ -98,8 +99,28 @@
     for name in there:
         pl.semaphore_signal(barrier, inc=1, device_id=there[name], device_id_type=MESH)
 
+    groups = 2 * tiles - 1
+
+    def row_shifts(side):
+        return range(HALO + 1, SPAN) if side else range(HALO)
+
     def tile(ref, lead, start, c):
         return ref[lead + (slice(start, start + SUB), slice(c * LANES, c * LANES + widths[c]))]
+
+    def zero_pads():
+        for c in range(tiles):
+            for f in range(nf):
+                for t in range(SPAN):
+                    sh[c, f, t, 0:SUB, :] = jnp.zeros((SUB, LANES), F32)
+                    sh[c, f, t, pl.ds(SUB + rows, SUB), :] = jnp.zeros((SUB, LANES), F32)
+        for n in range(nl // PIECES):
+            for m in range(groups):
+                for t in range(SPAN):
+                    tn[n, 0, m, t, 2 * SUB:3 * SUB, :] = jnp.zeros((SUB, LANES), F32)
+                    tn[n, 1, m, t, 0:SUB, :] = jnp.zeros((SUB, LANES), F32)
+        pw[...] = jnp.zeros(pw.shape, F32)
+
+    zero_pads()
 
     loads[0].wait()
     for k in range(blocks):
@@ -144,19 +165,6 @@
     for copy in loads[1:]:
         copy.wait()
 
-    def zero_pads():
-        for c in range(tiles):
-            for f in range(nf):
-                for t in range(SPAN):
-                    sh[c, f, t, 0:SUB, :] = jnp.zeros((SUB, LANES), F32)
-                    sh[c, f, t, pl.ds(SUB + rows, SUB), :] = jnp.zeros((SUB, LANES), F32)
-        for m in range(2 * tiles - 1):
-            for side in range(2):
-                for t in range(SPAN):
-                    tn[side, m, t, 0:SUB, :] = jnp.zeros((SUB, LANES), F32)
-                    tn[side, m, t, 2 * SUB:3 * SUB, :] = jnp.zeros((SUB, LANES), F32)
-        pw[...] = jnp.zeros(pw.shape, F32)
-
     def shifted(mid, left, right, t):
         d = t - HALO
         if d == 0:
@@ -168,10 +176,8 @@
             return jnp.where(lane >= LANES - d, 0.0, roll(mid, -d, 1))
         return roll(jnp.where(lane < d, right, mid), -d, 1)
 
-    def main():
-        zero_pads()
-
-        @pl.loop(0, nl)
+    def levels(begin, end):
+        @pl.loop(begin, end)
         def _(l):
             for c in range(tiles):
                 shape = (SUB, widths[c])
@@ -219,6 +225,20 @@
                     for k in range(blocks):
                         ov[f, l, c, pl.ds(k, SUB, stride=blocks), :] = acc[k]
 
+            for side in range(2):
+                for c in range(tiles):
+                    shifts = row_shifts(side)
+                    for n, i in enumerate([SPAN + t for t in range(SPAN)] + list(shifts)):
+                        x = rc[l, c, i, pl.ds(side * last, SUB), 0:widths[c]]
+                        x = jnp.concatenate([x, x], axis=-1) if c == tiles - 1 else x
+                        turned = roll(x, HALO, 0)
+                        x = jnp.where(sub < HALO, turned, x) if side else jnp.where(sub < HALO, x, turned)
+                        if i < SPAN:
+                            row = (sub & (HALO - 1)) + i
+                            x = jnp.where(row >= SPAN if side else row < HALO, x, 0.0)
+                        nw[l, side, c, n] = x
+
+    def spread():
         for side in range(2):
             for i in range(2 * SPAN):
                 for k in range(blocks):
@@ -227,113 +247,44 @@
                     x = x + roll(x, HALO * nl, 1)
                     pw[spot] = x + roll(x, 2 * HALO * nl, 1)
 
-    early = lax.rem(sector, EARLY_EVERY) == 0
-
-    @pl.when(early)
-    def _():
-        main()
-
+    place = lax.rem(sector, RUN)
+    ahead = jnp.where(place == 0, nl, jnp.where(place == 1, nl // 3, jnp.where(place == 2, nl // 6, 0)))
+    ahead = jnp.where(band + sector == 0, 0, ahead)
+    levels(0, ahead)
     pl.semaphore_wait(barrier, len(there))
     slot_n, slot_s = jnp.where(top, 0, 1), jnp.where(bottom, 1, 0)
-    sends = []
 
     def send(src, dst, i, j, to):
-        copy = pltpu.make_async_remote_copy(
+        return pltpu.make_async_remote_copy(
             src_ref=src, dst_ref=dst, send_sem=send_sem.at[i], recv_sem=recv_sem.at[j],
             device_id=there[to], device_id_type=MESH)
+
+    per = nl // PIECES
+    sends = []
+    for edge in range(2):
+        sends.append(send(strip.at[edge], strip_in.at[edge], edge, edge, "EW"[edge]))
+    for side, slot, row in ((0, slot_n, "N"), (1, slot_s, "S")):
+        for edge in range(2):
+            sends.append(send(corner.at[side, edge, pl.ds(0, HALO)], corner_in.at[slot, edge, pl.ds(0, HALO)],
+                              2 + 2 * side + edge, 2 + 2 * slot + edge, row + "EW"[edge]))
+    for q in range(PIECES):
+        piece = pl.ds(per * q, per)
+        for side, slot, to in ((0, slot_n, "N"), (1, slot_s, "S")):
+            sends.append(send(slab.at[side, piece], slab_in.at[slot, piece],
+                              6 + PIECES * side + q, 6 + PIECES * slot + q, to))
+    for copy in sends:
         copy.start()
-        sends.append(copy)
-
-    send(strip.at[0], strip_in.at[0], 0, 0, "E")
-    send(strip.at[1], strip_in.at[1], 1, 1, "W")
-    for side, slot, names in ((0, slot_n, ("NE", "NW")), (1, slot_s, ("SE", "SW"))):
-        for edge in range(2):
-            n = 2 * side + edge
-            send(corner.at[side, edge, pl.ds(0, HALO)], corner_in.at[slot, edge, pl.ds(0, HALO)], 2 + n, 2 + 2 * slot + edge, names[edge])
-    send(slab.at[0], slab_in.at[slot_n], 6, 6 + slot_n, "N")
-    send(slab.at[1], slab_in.at[slot_s], 7, 6 + slot_s, "S")
-
-    @pl.when(jnp.logical_not(early))
-    def _():
-        main()
+
+    levels(ahead, nl)
+    spread()
 
     def landed(ref, j):
         pltpu.make_async_copy(ref, ref, recv_sem.at[j]).wait()
 
-    landed(slab_in.at[0], 6)
-    landed(slab_in.at[1], 7)
-    group = sub & (HALO - 1)
-
-    def both(x, side):
-        return jnp.where(sub < HALO, x, roll(x, HALO, 0)) if side == 0 else jnp.where(sub < HALO, roll(x, HALO, 0), x)
-
-    @pl.loop(0, nl)
-    def _(l):
+    def columns(edge):
+        landed(strip_in.at[edge], edge)
         for side in range(2):
-            base = 0 if side == 0 else last
-            shifts = range(HALO) if side == 0 else range(HALO + 1, SPAN)
-            ends = [slab_in[side, l, 2 * tiles - 2]] * 2
-            ends[1] = roll(ends[1], -(LANES - tail), 1)
-            for m in range(2 * tiles - 1):
-                c, g = m // 2, m % 2
-                mid = slab_in[side, l, m]
-                for t in range(SPAN):
-                    d = t - HALO
-                    if c < tiles - 1:
-                        left = slab_in[side, l, m - 2] if c else None
-                        right = (slab_in[side, l, m + 2] if c + 2 < tiles else ends[g])
-                        x = shifted(mid, left, right, t)
-                    elif d <= 0:
-                        x = roll(mid, -d, 1)
-                        for h in range(2):
-                            lo = h * (LANES - tail)
-                            x = jnp.where((lane >= lo) & (lane < lo - d), roll(slab_in[side, l, m - 2 + h], lo - d, 1), x) if d else x
-                    else:
-                        inner = lane & (LANES // 2 - 1)
-                        x = jnp.where(inner >= LANES // 2 - d, 0.0, roll(mid, -d, 1))
-                    tn[side, m, t, SUB:2 * SUB, :] = x
-            for c in range(tiles):
-                def weight(i):
-                    x = rc[l, c, i, pl.ds(base, SUB), 0:widths[c]]
-                    if c == tiles - 1:
-                        x = jnp.concatenate([x, x], axis=-1)
-                    return both(x, side)
-
-                col_w = [weight(SPAN + t) for t in range(SPAN)]
-                row_w = {}
-                for s in shifts:
-                    valid = group + s < HALO if side == 0 else group + s >= SPAN
-                    row_w[s] = jnp.where(valid, weight(s), 0.0)
-                for g in range(2 if c < tiles - 1 else 1):
-                    m = 2 * c + g
-                    acc = None
-                    for s in shifts:
-                        first = SUB + s if side == 0 else s
-                        line = None
-                        for t in range(SPAN):
-                            term = col_w[t] * tn[side, m, t, pl.ds(first, SUB), :]
-                            line = term if line is None else line + term
-                        line = line * row_w[s]
-                        acc = line if acc is None else acc + line
-                    keep = sub < HALO if side == 0 else sub >= HALO
-                    for h in range(2 if c < tiles - 1 else 4):
-                        part = acc
-                        f = 2 * g + h if c < tiles - 1 else h
-                        if c == tiles - 1 and h >= 2:
-                            part = roll(part, -(LANES - tail), 1)
-                        if side == 0:
-                            part = part if f % 2 == 0 else roll(part, HALO, 0)
-                        else:
-                            part = part if f % 2 == 1 else roll(part, HALO, 0)
-                        spot = (f, l, c, pl.ds(base, SUB), slice(None))
-                        ov[spot] = ov[spot] + jnp.where(keep, part, 0.0)
-
-    landed(strip_in.at[0], 0)
-    landed(strip_in.at[1], 1)
-    for side in range(2):
-        for edge in range(2):
             landed(corner_in.at[side, edge, pl.ds(0, HALO)], 2 + 2 * side + edge)
-    for edge in range(2):
         taps = range(HALO) if edge == 0 else range(HALO + 1, SPAN)
         for t in taps:
             d = t if edge == 0 else t - SPAN
@@ -356,25 +307,79 @@
                 line = line * pw[edge, s, pl.ds(k, SUB, stride=blocks), :]
                 acc = line if acc is None else acc + line
             pd[edge, pl.ds(k, SUB, stride=blocks), :] = acc
-    copies = []
-    for f in range(nf):
-        for l in range(nl):
-            p = HALO * (f * nl + l)
-            for k in range(blocks):
-                at = pl.ds(SUB * k, SUB)
-                for c in range(tiles):
-                    x = ov[f, l, c, at, :]
-                    if c == 0:
-                        x = x + jnp.where(lane < HALO, roll(pd[0, at, :], -p, 1), 0.0)
-                    if c == tiles - 1:
-                        keep = (lane >= tail - HALO) & (lane < tail)
-                        x = x + jnp.where(keep, roll(pd[1, at, :], tail - HALO - p, 1), 0.0)
-                    fv[f, l, at, c * LANES:c * LANES + widths[c]] = x[:, :widths[c]]
-        copy = pltpu.make_async_copy(fv.at[f], out.at[f], out_sem.at[f])
-        copy.start()
-        copies.append(copy)
-    for copy in copies:
-        copy.wait()
+        for k in range(blocks):
+            at = pl.ds(SUB * k, SUB)
+            extra = pd[edge, at, :]
+            for f in range(nf):
+                for l in range(nl):
+                    p = HALO * (f * nl + l)
+                    if edge == 0:
+                        x = ov[f, l, 0, at, :]
+                        out[f, l, at, 0:LANES] = x + jnp.where(lane < HALO, roll(extra, -p, 1), 0.0)
+                        continue
+                    for c in range(1, tiles):
+                        x = ov[f, l, c, at, :]
+                        if c == tiles - 1:
+                            keep = (lane >= tail - HALO) & (lane < tail)
+                            x = x + jnp.where(keep, roll(extra, tail - HALO - p, 1), 0.0)
+                        out[f, l, at, c * LANES:c * LANES + widths[c]] = x[:, :widths[c]]
+
+    columns(1)
+    for l in range(nl):
+        if l % per == 0:
+            for side in range(2):
+                landed(slab_in.at[side, pl.ds(l, per)], 6 + PIECES * side + l // per)
+        for side in range(2):
+            buf = tn.at[l % per, side]
+            base = side * last
+            ends = [slab_in[side, l, groups - 1]] * 2
+            ends[1] = roll(ends[1], -tail, 1)
+            for m in range(groups):
+                c, g = m // 2, m % 2
+                mid = slab_in[side, l, m]
+                for t in range(SPAN):
+                    d = t - HALO
+                    if c < tiles - 1:
+                        left = slab_in[side, l, m - 2] if c else None
+                        right = slab_in[side, l, m + 2] if c + 2 < tiles else ends[g]
+                        x = shifted(mid, left, right, t)
+                    elif d <= 0:
+                        x = roll(mid, -d, 1)
+                        for h in range(2):
+                            lo = h * tail
+                            edge = roll(slab_in[side, l, m - 2 + h], lo - d, 1)
+                            x = jnp.where((lane >= lo) & (lane < lo - d), edge, x) if d else x
+                    else:
+                        x = jnp.where((lane & (tail - 1)) >= tail - d, 0.0, roll(mid, -d, 1))
+                    buf[m, t, SUB:2 * SUB, :] = x
+            for c in range(tiles):
+                shifts = row_shifts(side)
+                col_w = [nw[l, side, c, t] for t in range(SPAN)]
+                row_w = [nw[l, side, c, SPAN + n] for n in range(len(shifts))]
+                for g in range(2 if c < tiles - 1 else 1):
+                    m = 2 * c + g
+                    acc = None
+                    for n, s in enumerate(shifts):
+                        start = SUB + s if side == 0 else s
+                        line = None
+                        for t in range(SPAN):
+                            term = col_w[t] * buf[m, t, pl.ds(start, SUB), :]
+                            line = term if line is None else line + term
+                        line = line * row_w[n]
+                        acc = line if acc is None else acc + line
+                    keep = sub < HALO if side == 0 else sub >= HALO
+                    for h in range(2 if c < tiles - 1 else 4):
+                        f = 2 * g + h if c < tiles - 1 else h
+                        part = roll(acc, -tail, 1) if h >= 2 else acc
+                        part = part if f % 2 == side else roll(part, HALO, 0)
+                        part = jnp.where(keep, part, 0.0)
+                        if c == 0:
+                            spot = (f, l, c, pl.ds(base, SUB), slice(None))
+                            ov[spot] = ov[spot] + part
+                        else:
+                            spot = (f, l, pl.ds(base, SUB), slice(c * LANES, c * LANES + widths[c]))
+                            out[spot] = out[spot] + part[:, :widths[c]]
+    columns(0)
     for copy in sends:
         copy.wait_send()
 
@@ -392,7 +397,7 @@
             functools.partial(kernel, dims),
             out_shape=jax.ShapeDtypeStruct(fields.shape, F32),
             in_specs=[pl.BlockSpec(memory_space=pltpu.HBM)] * 4,
-            out_specs=pl.BlockSpec(memory_space=pltpu.HBM),
+            out_specs=pl.BlockSpec(memory_space=pltpu.VMEM),
             scratch_shapes=[
                 vmem(nf, nl, rows, cols),
                 pltpu.VMEM((nl, rows, cols), jnp.int32),
@@ -404,17 +409,18 @@
                 vmem(2, nl, groups, SUB, LANES), vmem(2, nl, groups, SUB, LANES),
                 vmem(2, rows, LANES), vmem(2, rows, LANES),
                 vmem(2, 2, SUB, LANES), vmem(2, 2, SUB, LANES),
-                vmem(2, groups, SPAN, 3 * SUB, LANES),
+                vmem(nl // PIECES, 2, groups, SPAN, 3 * SUB, LANES),
+                vmem(nl, 2, tiles, SPAN + HALO, SUB, LANES),
                 vmem(2, SPAN, rows + 2 * SUB, LANES),
                 vmem(2, 2 * SPAN, rows, LANES),
                 vmem(2, rows, LANES),
-                pltpu.SemaphoreType.DMA((4,)), pltpu.SemaphoreType.DMA((nf,)),
-                pltpu.SemaphoreType.DMA((8,)), pltpu.SemaphoreType.DMA((8,)),
+                pltpu.SemaphoreType.DMA((4,)),
+                pltpu.SemaphoreType.DMA((6 + 2 * PIECES,)), pltpu.SemaphoreType.DMA((6 + 2 * PIECES,)),
             ],
             compiler_params=pltpu.CompilerParams(
-                collective_id=0, has_side_effects=True, vmem_limit_bytes=67043328),
+                collective_id=0, has_side_effects=True, vmem_limit_bytes=40 << 20),
             name="advect",
-        )(fields, dep_row, dep_col, weights)
+        )(*[pltpu.with_memory_space_constraint(x, pltpu.HBM) for x in (fields, dep_row, dep_col, weights)])
 
     return jax.shard_map(
         body,

time: 30.4 us -> 24.1 us (0.79)
  the two profiles are of different devices: /device:TPU:4 before, /device:TPU:57 now
where the time goes in v2:
time: 24.1 us; the launch traced here: 24 us
  Pallas kernels  23 us (95%)
  local copies, waits for them, and re-layouts  1.02 us (4%)
    pallas_call x1, Pallas kernels, body(): pl.pallas_call(functools.partial(kernel, dims), out_shape=jax.ShapeDtypeS...  23 us
    unnamed x1, local copies, waits for them, and re-layouts  1.02 us

profile of v2, /device:TPU:57, one launch (start us, length us, event | category | flops | bytes accessed | tf_op | source)
XLA Modules:
  0.0 24.0 jit_solution(9453452911203399931)
XLA Ops:
  0.0 23.0 %advect.1 = f32[4,6,32,320]{3,2,1,0:T(8,128)S(1)} custom-call(f32[4,6,32,320]{3,2,1,0:T(8,128)} %fields.1, s32[6,32,320]{2,1,0:T(8,128)} %dep_row.1, s32[6,32,320]{2,1,0:T(8,128)} %dep_col.1, f32[8,6,32,320]{3,2,1,0:T(8,128)} %weights.1), custom_call_target="tpu_custom_call" | custom-call | tf_op jit(solution)/shard_map/advect/pallas_call | solution.py:396
  23.0 1.0 %copy.6 = f32[4,6,32,320]{3,2,1,0:T(8,128)} copy(f32[4,6,32,320]{3,2,1,0:T(8,128)S(1)} %advect.1) | data formatting | bytes 1966080

commit v3 on v2

--- a/solution.py
+++ b/solution.py
@@ -14,7 +14,7 @@
 HALO = 4
 SPAN = 2 * HALO
 RUN = 4
-PIECES = 3
+PIECES = 6
 
 
 def lane_iota(shape):

time: 24.1 us -> 24 us (level)
  no operation moved by 1% of the time
where the time goes in v3:
time: 24 us; the launch traced here: 23.9 us
  Pallas kernels  22.8 us (95%)
  local copies, waits for them, and re-layouts  1.02 us (4%)
    pallas_call x1, Pallas kernels, body(): pl.pallas_call(functools.partial(kernel, dims), out_shape=jax.ShapeDtypeS...  22.8 us
    unnamed x1, local copies, waits for them, and re-layouts  1.02 us

profile of v3, /device:TPU:57, one launch (start us, length us, event | category | flops | bytes accessed | tf_op | source)
XLA Modules:
  0.0 23.9 jit_solution(4709091267895347988)
XLA Ops:
  0.0 22.8 %advect.1 = f32[4,6,32,320]{3,2,1,0:T(8,128)S(1)} custom-call(f32[4,6,32,320]{3,2,1,0:T(8,128)} %fields.1, s32[6,32,320]{2,1,0:T(8,128)} %dep_row.1, s32[6,32,320]{2,1,0:T(8,128)} %dep_col.1, f32[8,6,32,320]{3,2,1,0:T(8,128)} %weights.1), custom_call_target="tpu_custom_call" | custom-call | tf_op jit(solution)/shard_map/advect/pallas_call | solution.py:396
  22.8 1.0 %copy.6 = f32[4,6,32,320]{3,2,1,0:T(8,128)} copy(f32[4,6,32,320]{3,2,1,0:T(8,128)S(1)} %advect.1) | data formatting | bytes 1966080
